TPU v7x, 32 devices: a whole 2x2x4 slice. The times are simulated.
32 devices in a mesh: dp: 16 (over z, x, core), tensor: 2 (over y).
Axes of the slice: x: 2, y: 2, z: 4, core: 2. Of those that a mesh axis runs over, the one named last changes fastest.
Arguments:
- inputs: bfloat16 [2, 16, 1024, 768], P(None, 'dp', 'tensor'), may hold values from -6 to 6
- seg_ids: int32 [2, 16, 1024], P(None, 'dp'), may hold values from 0 to 7, never falling along the last dimension, each value on 1 to 512 neighbouring positions
- keep_mask: int32 [2, 16, 1024], P(None, 'dp'), may hold values 0 or 1
- w_qkv: bfloat16 [3, 768, 768], P(None, 'dp', 'tensor'), may hold values from -0.21875 to 0.21875
- b_qv: float32 [2, 768], replicated, may hold values from -3 to 3
- w_o: bfloat16 [768, 768], P('tensor', 'dp'), may hold values from -1.75 to 1.75
- b_o: float32 [768], replicated, may hold values from -3 to 3
- gain_one: float32 [768], replicated, may hold values from 0.5 to 1.5
- shift_one: float32 [768], replicated, may hold values from -3 to 3
- w_up: bfloat16 [768, 3072], P('dp', 'tensor'), may hold values from -0.21875 to 0.21875
- b_up: float32 [3072], replicated, may hold values from -3 to 3
- w_down: bfloat16 [3072, 768], P('tensor', 'dp'), may hold values from -0.109375 to 0.109375
- b_down: float32 [768], replicated, may hold values from -3 to 3
- gain_two: float32 [768], replicated, may hold values from 0.5 to 1.5
- shift_two: float32 [768], replicated, may hold values from -3 to 3
- out_grad: bfloat16 [2, 16, 1024, 768], P(None, 'dp', 'tensor'), may hold values from -6 to 6
Outputs:
- out: bfloat16 [2, 16, 1024, 768], P(None, 'dp', 'tensor')
- x_grad: float32 [2, 16, 1024, 768], P(None, 'dp', 'tensor')
- w_qkv_grad: float32 [3, 768, 768], P(None, 'dp', 'tensor')
- b_qv_grad: float32 [2, 768], P(None, 'tensor')
- w_o_grad: float32 [768, 768], P('tensor', 'dp')
- b_o_grad: float32 [768], replicated
- gain_one_grad: float32 [768], replicated
- shift_one_grad: float32 [768], replicated
- w_up_grad: float32 [768, 3072], P('dp', 'tensor')
- b_up_grad: float32 [3072], P('tensor')
- w_down_grad: float32 [3072, 768], P('tensor', 'dp')
- b_down_grad: float32 [768], replicated
- gain_two_grad: float32 [768], replicated
- shift_two_grad: float32 [768], replicated
Inputs may be any that keep to these rules, and one draw needn't show every extreme that they name: `seg_ids`: within each sequence of 1024 positions the document numbers never fall; each document holds 1 to 512 positions and one holds exactly 512.
All inputs are finite; a program needn't handle non-finite values. No bound on the sum of `keep_mask` on one device may be relied on, other than what follows from the above.
Results may differ from a plain program's by a relative error of at most 0.015.
Values may be sent and summed in bfloat16 or wider, within the bound.
A program may use at most 192 MiB of HBM per device.

v0:
```python
import math
import jax
import jax.numpy as jnp
from jax import lax
from jax.sharding import PartitionSpec as P

HEAD_DIM = 64
EPS = 1e-06


def gelu_exact(v):
    return 0.5 * v * (1.0 + lax.erf(v * 0.7071067811865476))


def gelu_slope(v):
    return (
        0.5 * (1.0 + lax.erf(v * 0.7071067811865476))
        + v * jnp.exp(-0.5 * v * v) * 0.3989422804014327
    )


def norm_rows(v, gain, shift):
    row_mean = jnp.mean(v, axis=-1, keepdims=True)
    centered = v - row_mean
    factor = lax.rsqrt(jnp.mean(centered * centered, axis=-1, keepdims=True) + EPS)
    normed = centered * factor
    return (normed * gain + shift, normed, factor)


def norm_back(grad_rows, normed, factor, gain):
    inner = grad_rows * gain
    return factor * (
        inner
        - jnp.mean(inner, axis=-1, keepdims=True)
        - normed * jnp.mean(inner * normed, axis=-1, keepdims=True)
    )


def allowed_keys(seg_block, seg_full, keep_full, row_start):
    shape_pair = (seg_block.shape[0], seg_full.shape[0])
    own_pos = row_start + lax.broadcasted_iota(jnp.int32, shape_pair, 0)
    key_pos = lax.broadcasted_iota(jnp.int32, shape_pair, 1)
    return (seg_block[:, None] == seg_full[None, :]) & (
        (keep_full[None, :] == 1) | (own_pos == key_pos)
    )


def block_scores(q_rows, key_rows, allowed, score_scale):
    raw = (
        jnp.einsum("qhd,khd->hqk", q_rows, key_rows, preferred_element_type=jnp.float32)
        * score_scale
    )
    return jnp.where(allowed[None], raw, -1e30)


def attend(queries, key_rows, values, seg_full, keep_full, score_scale, block_rows):
    length, head_count, head_width = queries.shape
    block_count = length // block_rows
    starts = jnp.arange(block_count, dtype=jnp.int32) * block_rows

    def per_block(block_item):
        q_rows, seg_block, row_start = block_item
        scores = block_scores(
            q_rows, key_rows, allowed_keys(seg_block, seg_full, keep_full, row_start), score_scale
        )
        row_max = jnp.max(scores, axis=-1, keepdims=True)
        exps_rows = jnp.exp(scores - row_max)
        denom = jnp.sum(exps_rows, axis=-1, keepdims=True)
        low_probs = (exps_rows / denom).astype(jnp.bfloat16)
        context = jnp.einsum("hqk,khd->qhd", low_probs, values, preferred_element_type=jnp.float32)
        return (context.astype(jnp.bfloat16), (row_max + jnp.log(denom))[..., 0])

    context, logsum = lax.map(
        per_block,
        (
            queries.reshape(block_count, block_rows, head_count, head_width),
            seg_full.reshape(block_count, block_rows),
            starts,
        ),
    )
    return (context.reshape(length, head_count * head_width), logsum)


def attend_back(
    queries, key_rows, values, grad_context, logsum, seg_full, keep_full, score_scale, block_rows
):
    length, head_count, head_width = queries.shape
    block_count = length // block_rows
    starts = jnp.arange(block_count, dtype=jnp.int32) * block_rows

    def per_block(carried, block_item):
        key_acc, value_acc = carried
        q_rows, g_rows, lse_rows, seg_block, row_start = block_item
        scores = block_scores(
            q_rows, key_rows, allowed_keys(seg_block, seg_full, keep_full, row_start), score_scale
        )
        probs = jnp.exp(scores - lse_rows[..., None])
        low_probs = probs.astype(jnp.bfloat16)
        grad_probs = jnp.einsum("qhd,khd->hqk", g_rows, values, preferred_element_type=jnp.float32)
        inner = jnp.sum(probs * grad_probs, axis=-1, keepdims=True)
        grad_scores = (probs * (grad_probs - inner)).astype(jnp.bfloat16)
        grad_q = (
            jnp.einsum("hqk,khd->qhd", grad_scores, key_rows, preferred_element_type=jnp.float32)
            * score_scale
        )
        key_acc = (
            key_acc
            + jnp.einsum("hqk,qhd->khd", grad_scores, q_rows, preferred_element_type=jnp.float32)
            * score_scale
        )
        value_acc = value_acc + jnp.einsum(
            "hqk,qhd->khd", low_probs, g_rows, preferred_element_type=jnp.float32
        )
        return ((key_acc, value_acc), grad_q.astype(jnp.bfloat16))

    zero_grad = jnp.zeros((length, head_count, head_width), jnp.float32)
    grad_ctx4 = grad_context.reshape(block_count, block_rows, head_count, head_width)
    (key_acc, value_acc), grad_q = lax.scan(
        per_block,
        (zero_grad, zero_grad),
        (
            queries.reshape(block_count, block_rows, head_count, head_width),
            grad_ctx4,
            logsum,
            seg_full.reshape(block_count, block_rows),
            starts,
        ),
    )
    flat = head_count * head_width
    return (
        grad_q.reshape(length, flat),
        key_acc.reshape(length, flat).astype(jnp.bfloat16),
        value_acc.reshape(length, flat).astype(jnp.bfloat16),
    )


def add_all(left, right):
    return tuple((a + b for a, b in zip(left, right)))


def shards(
    inputs,
    seg_ids,
    keep_mask,
    w_qkv,
    b_qv,
    w_o,
    b_o,
    gain_one,
    shift_one,
    w_up,
    b_up,
    w_down,
    b_down,
    gain_two,
    shift_two,
    out_grad,
):
    micro_count = inputs.shape[0]
    own_count = inputs.shape[2]
    half_width = w_qkv.shape[2]
    half_units = w_up.shape[1]
    score_scale = 1.0 / math.sqrt(HEAD_DIM)
    tensor_count = lax.axis_size("tensor")
    tensor_rank = lax.axis_index("tensor")
    length = own_count * tensor_count
    block_rows = min(512, length)
    bias_qv = lax.dynamic_slice_in_dim(b_qv, tensor_rank * half_width, half_width, 1)
    bias_up = lax.dynamic_slice_in_dim(b_up, tensor_rank * half_units, half_units, 0)
    shard_grads = None
    local_totals = None
    small_totals = None
    out_list = []
    grad_list = []
    for micro_index in range(micro_count):
        own_rows = inputs[micro_index, 0]
        seg_full = seg_ids[micro_index, 0]
        keep_full = keep_mask[micro_index, 0]
        full_qkv = lax.all_gather(w_qkv, "dp", axis=1, tiled=True)
        full_o = lax.all_gather(w_o, "dp", axis=1, tiled=True)
        full_up = lax.all_gather(w_up, "dp", axis=0, tiled=True)
        full_down = lax.all_gather(w_down, "dp", axis=1, tiled=True)
        head_count = full_qkv.shape[2] // HEAD_DIM
        gathered = lax.all_gather(own_rows, "tensor", axis=0, tiled=True)
        projected = jnp.einsum(
            "ld,cde->cle", gathered, full_qkv, preferred_element_type=jnp.float32
        )
        bias_rows = jnp.stack([bias_qv[0], jnp.zeros_like(bias_qv[0]), bias_qv[1]])
        projected = (projected + bias_rows[:, None, :]).astype(jnp.bfloat16)
        queries = projected[0].reshape(length, head_count, HEAD_DIM)
        key_rows = projected[1].reshape(length, head_count, HEAD_DIM)
        values = projected[2].reshape(length, head_count, HEAD_DIM)
        context, logsum = attend(
            queries, key_rows, values, seg_full, keep_full, score_scale, block_rows
        )
        attn_rows = lax.psum_scatter(
            jnp.dot(context, full_o, preferred_element_type=jnp.float32),
            "tensor",
            scatter_dimension=0,
            tiled=True,
        )
        first_sum = own_rows.astype(jnp.float32) + attn_rows + b_o
        hidden, normed_one, factor_one = norm_rows(first_sum, gain_one, shift_one)
        hidden_low = hidden.astype(jnp.bfloat16)
        spread = lax.all_gather(hidden_low, "tensor", axis=0, tiled=True)
        upward = jnp.dot(spread, full_up, preferred_element_type=jnp.float32) + bias_up
        active = gelu_exact(upward).astype(jnp.bfloat16)
        ffn_rows = lax.psum_scatter(
            jnp.dot(active, full_down, preferred_element_type=jnp.float32),
            "tensor",
            scatter_dimension=0,
            tiled=True,
        )
        second_sum = hidden + ffn_rows + b_down
        result, normed_two, factor_two = norm_rows(second_sum, gain_two, shift_two)
        grad_out = out_grad[micro_index, 0].astype(jnp.float32)
        sum_g2 = jnp.sum(grad_out * normed_two, axis=0)
        sum_e2 = jnp.sum(grad_out, axis=0)
        grad_second = norm_back(grad_out, normed_two, factor_two, gain_two)
        sum_down = jnp.sum(grad_second, axis=0)
        second_low = grad_second.astype(jnp.bfloat16)
        grad_ffn = lax.all_gather(second_low, "tensor", axis=0, tiled=True)
        local_down = lax.dot_general(
            active, grad_ffn, (((0,), (0,)), ((), ())), preferred_element_type=jnp.float32
        )
        grad_active = lax.dot_general(
            grad_ffn, full_down, (((1,), (1,)), ((), ())), preferred_element_type=jnp.float32
        )
        grad_up = (grad_active * gelu_slope(upward)).astype(jnp.bfloat16)
        sum_up = jnp.sum(grad_up.astype(jnp.float32), axis=0)
        local_up = lax.dot_general(
            spread, grad_up, (((0,), (0,)), ((), ())), preferred_element_type=jnp.float32
        )
        grad_hidden = grad_second + lax.psum_scatter(
            lax.dot_general(
                grad_up, full_up, (((1,), (1,)), ((), ())), preferred_element_type=jnp.float32
            ),
            "tensor",
            scatter_dimension=0,
            tiled=True,
        )
        sum_g1 = jnp.sum(grad_hidden * normed_one, axis=0)
        sum_e1 = jnp.sum(grad_hidden, axis=0)
        grad_first = norm_back(grad_hidden, normed_one, factor_one, gain_one)
        sum_o = jnp.sum(grad_first, axis=0)
        first_low = grad_first.astype(jnp.bfloat16)
        grad_attn = lax.all_gather(first_low, "tensor", axis=0, tiled=True)
        local_o = lax.dot_general(
            context, grad_attn, (((0,), (0,)), ((), ())), preferred_element_type=jnp.float32
        )
        grad_context = lax.dot_general(
            grad_attn, full_o, (((1,), (1,)), ((), ())), preferred_element_type=jnp.float32
        ).astype(jnp.bfloat16)
        grad_q, grad_k, grad_v = attend_back(
            queries,
            key_rows,
            values,
            grad_context,
            logsum,
            seg_full,
            keep_full,
            score_scale,
            block_rows,
        )
        grad_proj = jnp.stack([grad_q, grad_k, grad_v])
        sum_qv = jnp.stack(
            [
                jnp.sum(grad_q.astype(jnp.float32), axis=0),
                jnp.sum(grad_v.astype(jnp.float32), axis=0),
            ]
        )
        local_qkv = jnp.einsum(
            "ld,cle->cde", gathered, grad_proj, preferred_element_type=jnp.float32
        )
        x_rows = grad_first + lax.psum_scatter(
            jnp.einsum(
                "cle,cde->ld", grad_proj, full_qkv, preferred_element_type=jnp.float32
            ).astype(jnp.bfloat16),
            "tensor",
            scatter_dimension=0,
            tiled=True,
        ).astype(jnp.float32)
        smalls = (sum_qv, sum_o, sum_g1, sum_e1, sum_up, sum_down, sum_g2, sum_e2)
        result, x_rows, local_grads, smalls = (
            result.astype(jnp.bfloat16),
            x_rows,
            (local_qkv, local_o, local_up, local_down),
            smalls,
        )
        out_list.append(result)
        grad_list.append(x_rows)
        small_totals = smalls if small_totals is None else add_all(small_totals, smalls)
        take_shard_grads = shard_grads
        settled = (
            lax.psum_scatter(local_grads[0], "dp", scatter_dimension=1, tiled=True),
            lax.psum_scatter(local_grads[1], "dp", scatter_dimension=1, tiled=True),
            lax.psum_scatter(local_grads[2], "dp", scatter_dimension=0, tiled=True),
            lax.psum_scatter(local_grads[3], "dp", scatter_dimension=1, tiled=True),
        )
        take_shard_grads = (
            settled if take_shard_grads is None else add_all(take_shard_grads, settled)
        )
        shard_grads, local_totals = (take_shard_grads, local_totals)
    out_rows = jnp.stack(out_list)[:, None]
    grad_rows = jnp.stack(grad_list)[:, None]
    qv_full = lax.dynamic_update_slice(
        jnp.zeros((2, half_width * tensor_count), jnp.float32),
        small_totals[0],
        (jnp.int32(0), tensor_rank * half_width),
    )
    up_full = lax.dynamic_update_slice(
        jnp.zeros((half_units * tensor_count,), jnp.float32),
        small_totals[4],
        (tensor_rank * half_units,),
    )
    summed = lax.psum(
        (
            qv_full,
            small_totals[1],
            small_totals[2],
            small_totals[3],
            up_full,
            small_totals[5],
            small_totals[6],
            small_totals[7],
        ),
        ("dp", "tensor"),
    )
    grad_qv = lax.dynamic_slice_in_dim(summed[0], tensor_rank * half_width, half_width, 1)
    grad_up_bias = lax.dynamic_slice_in_dim(summed[4], tensor_rank * half_units, half_units, 0)
    return (
        out_rows,
        grad_rows,
        shard_grads[0],
        grad_qv,
        shard_grads[1],
        summed[1],
        summed[2],
        summed[3],
        shard_grads[2],
        grad_up_bias,
        shard_grads[3],
        summed[5],
        summed[6],
        summed[7],
    )


def solution(mesh):
    placed = (
        P(None, "dp", "tensor", None),
        P(None, "dp", None),
        P(None, "dp", None),
        P(None, "dp", "tensor"),
        P(),
        P("tensor", "dp"),
        P(),
        P(),
        P(),
        P("dp", "tensor"),
        P(),
        P("tensor", "dp"),
        P(),
        P(),
        P(),
        P(None, "dp", "tensor", None),
    )
    return jax.shard_map(
        shards,
        mesh=mesh,
        in_specs=placed,
        out_specs=(
            P(None, "dp", "tensor", None),
            P(None, "dp", "tensor", None),
            P(None, "dp", "tensor"),
            P(None, "tensor"),
            P("tensor", "dp"),
            P(),
            P(),
            P(),
            P("dp", "tensor"),
            P("tensor"),
            P("tensor", "dp"),
            P(),
            P(),
            P(),
        ),
        check_vma=False,
    )
```

profile of v0, /device:TPU:0, one launch (start us, length us, event | category | flops | bytes accessed | tf_op | source)
XLA Modules:
  0.0 1215.2 jit_solution(6514101610812780588)
XLA Ops:
  11.5 24.9 %all_gather.42 = bf16[384,768]{0,1:T(8,128)(2,1)S(1)} all-gather(bf16[384,48]{0,1:T(8,128)(2,1)S(1)} %copy-done.58), channel_id=1, replica_groups=mesh['dp'=16,'tensor'=2] {'dp'}, dimensions={1}, use_global_device_ids=true | all-gather | bytes 626688 | tf_op jit(solution)/shard_map/all_gather | solution.py:180
  40.1 42.8 %all-gather.14.cloned.1.call-done = bf16[3,768,384]{2,1,0:T(8,128)(2,1)} async-done(((bf16[3,48,384]{2,1,0:T(8,128)(2,1)}), bf16[3,768,384]{2,1,0:T(8,128)(2,1)}) %all-gather.14.cloned.1.call-update) | async-done | bytes 1769488 | tf_op jit(solution)/shard_map/all_gather | solution.py:179
  90.9 26.0 %while.55 = (s32[]{:T(128)}, bf16[2,512,6,64]{1,3,2,0:T(8,128)(2,1)}, f32[2,6,512]{2,1,0:T(8,128)S(1)}, s32[2,512]{1,0:T(2,128)S(1)}, s32[1,1,1024]{2,1,0:T(1,12...) while((s32[]{:T(128)}, ...), condition=%wide.region_13.14_spmd, body=%wide.region_10.13_spmd.sunk | while | flops 845347328 | bytes 42336904 | solution.py:73
  132.2 26.0 %while.54 = (s32[]{:T(128)}, bf16[2,512,6,64]{1,3,2,0:T(8,128)(2,1)}, f32[2,6,512]{2,1,0:T(8,128)S(1)}, s32[2,512]{1,0:T(2,128)S(1)}, s32[1,1,1024]{2,1,0:T(1,12...) while((s32[]{:T(128)}, ...), condition=%wide.region_3.4_spmd, body=%wide.region_0.3_spmd.sunk | while | flops 845347328 | bytes 42336904 | solution.py:73
  165.5 46.1 %reduce-scatter.12.cloned.1.call-done = f32[512,768]{1,0:T(8,128)} async-done(((f32[1024,768]{1,0:T(8,128)}), f32[512,768]{1,0:T(8,128)}) %reduce-scatter.12.cloned.1.call-update) | async-done | bytes 1572880 | tf_op jit(solution)/shard_map/reduce_scatter | solution.py:196
  218.6 37.5 %all-gather.18.cloned.1.call-done = bf16[768,1536]{1,0:T(8,128)(2,1)} async-done(((bf16[48,1536]{1,0:T(8,128)(2,1)}), bf16[768,1536]{1,0:T(8,128)(2,1)}) %all-gather.18.cloned.1.call-update) | async-done | bytes 2359312 | tf_op jit(solution)/shard_map/all_gather | solution.py:181
  256.1 27.5 %all-gather.22.cloned.1.call-done = bf16[1024,768]{1,0:T(8,128)(2,1)} async-done(((bf16[512,768]{1,0:T(8,128)(2,1)}), bf16[1024,768]{1,0:T(8,128)(2,1)}) %all-gather.22.cloned.1.call-update) | async-done | bytes 1572880 | tf_op jit(solution)/shard_map/all_gather | solution.py:205
  283.6 7.4 fusion.149
  291.0 21.9 %all-gather.16.cloned.1.call-done = bf16[1024,768]{1,0:T(8,128)(2,1)} async-done(((bf16[512,768]{1,0:T(8,128)(2,1)}), bf16[1024,768]{1,0:T(8,128)(2,1)}) %all-gather.16.cloned.1.call-update) | async-done | bytes 1572880 | tf_op jit(solution)/shard_map/all_gather | solution.py:205
  312.9 11.0 multiply_convert_fusion.3
  324.0 33.6 %all-gather.20.cloned.1.call-done = bf16[1536,768]{0,1:T(8,128)(2,1)} async-done(((bf16[1536,48]{0,1:T(8,128)(2,1)}), bf16[1536,768]{0,1:T(8,128)(2,1)}) %all-gather.20.cloned.1.call-update) | async-done | bytes 2359312 | tf_op jit(solution)/shard_map/all_gather | solution.py:182
  357.6 6.9 fusion.147
  364.5 6.9 fusion.150
  371.5 35.3 %reduce-scatter.14.cloned.1.call-done = f32[512,768]{1,0:T(8,128)} async-done(((f32[1024,768]{1,0:T(8,128)}), f32[512,768]{1,0:T(8,128)}) %reduce-scatter.14.cloned.1.call-update) | async-done | bytes 1572880 | tf_op jit(solution)/shard_map/reduce_scatter | solution.py:208
  406.8 45.7 %reduce-scatter.18.cloned.1.call-done = f32[512,768]{1,0:T(8,128)} async-done(((f32[1024,768]{1,0:T(8,128)}), f32[512,768]{1,0:T(8,128)}) %reduce-scatter.18.cloned.1.call-update) | async-done | bytes 1572880 | tf_op jit(solution)/shard_map/reduce_scatter | solution.py:208
  467.6 24.7 %all-gather.24.cloned.1.call-done = bf16[1024,768]{1,0:T(8,128)(2,1)} async-done(((bf16[512,768]{1,0:T(8,128)(2,1)}), bf16[1024,768]{1,0:T(8,128)(2,1)}) %all-gather.24.cloned.1.call-update) | async-done | bytes 1572880 | tf_op jit(solution)/shard_map/all_gather | solution.py:222
  492.2 7.7 convert_reduce_fusion.1
  505.9 15.0 %all-gather.28.cloned.1.call-done = bf16[1024,768]{1,0:T(8,128)(2,1)} async-done(((bf16[512,768]{1,0:T(8,128)(2,1)}), bf16[1024,768]{1,0:T(8,128)(2,1)}) %all-gather.28.cloned.1.call-update) | async-done | bytes 1572880 | tf_op jit(solution)/shard_map/all_gather | solution.py:222
  521.0 7.7 convert_reduce_fusion
  534.7 31.8 %reduce-scatter.20.cloned.1.call-done = f32[512,768]{1,0:T(8,128)} async-done(((f32[1024,768]{1,0:T(8,128)}), f32[512,768]{1,0:T(8,128)}) %reduce-scatter.20.cloned.1.call-update) | async-done | bytes 1572880 | tf_op jit(solution)/shard_map/reduce_scatter | solution.py:234
  571.3 40.8 %reduce-scatter.24.cloned.1.call-done = f32[512,768]{1,0:T(8,128)} async-done(((f32[1024,768]{1,0:T(8,128)}), f32[512,768]{1,0:T(8,128)}) %reduce-scatter.24.cloned.1.call-update) | async-done | bytes 1572880 | tf_op jit(solution)/shard_map/reduce_scatter | solution.py:234
  624.0 22.5 %all-gather.26.cloned.1.call-done = bf16[1024,768]{1,0:T(8,128)(2,1)} async-done(((bf16[512,768]{1,0:T(8,128)(2,1)}), bf16[1024,768]{1,0:T(8,128)(2,1)}) %all-gather.26.cloned.1.call-update) | async-done | bytes 1572880 | tf_op jit(solution)/shard_map/all_gather | solution.py:247
  651.7 65.0 %while.56 = (s32[]{:T(128)}, f32[1024,6,64]{0,2,1:T(8,128)}, f32[1024,6,64]{0,2,1:T(8,128)}, bf16[2,512,6,64]{1,3,2,0:T(8,128)(2,1)}, bf16[2,512,6,64]{1,3,2,0:T...) while((s32[]{:T(128)}, f32[1024,6,64]{0,2,1:T(8,128)}, ...), condition=%wide.region_27.28_spmd.clone, body=%wide.region_25.27_spmd.clone.sunk | while | flops 2064906752 | bytes 211006768 | solution.py:118
  655.8 6.3 multiply_reduce_fusion.14
  662.1 5.0 multiply_convert_fusion.6
  667.1 5.3 bitcast_add_fusion.8
  672.4 6.2 fusion.269
  687.4 6.3 multiply_reduce_fusion.14
  698.7 5.7 bitcast_add_fusion.8
  704.5 6.2 fusion.269
  710.7 6.0 bitcast_add_fusion.9
  725.1 65.3 %while.57 = (s32[]{:T(128)}, f32[1024,6,64]{0,2,1:T(8,128)}, f32[1024,6,64]{0,2,1:T(8,128)}, bf16[2,512,6,64]{1,3,2,0:T(8,128)(2,1)}, bf16[2,512,6,64]{1,3,2,0:T...) while((s32[]{:T(128)}, f32[1024,6,64]{0,2,1:T(8,128)}, ...), condition=%wide.region_36.37_spmd.clone, body=%wide.region_34.36_spmd.clone.sunk | while | flops 2064906752 | bytes 211006768 | solution.py:118
  729.4 6.3 multiply_reduce_fusion.15
  740.7 5.3 bitcast_add_fusion.10
  746.0 6.2 fusion.281
  761.0 6.3 multiply_reduce_fusion.15
  772.3 5.8 bitcast_add_fusion.10
  778.1 6.2 fusion.281
  784.2 6.0 bitcast_add_fusion.11
  814.9 5.2 bitcast_convert_fusion.1
  820.4 5.2 bitcast_convert_fusion
  857.5 41.0 %all-reduce.1 = (f32[2,768]{1,0:T(2,128)S(1)}, f32[768]{0:T(1024)}, f32[768]{0:T(1024)}, f32[768]{0:T(1024)}, f32[3072]{0:T(1024)S(1)}, /*index=5*/f32[768]{0:T(1024)}, f32[768]{0:T(1024)}, f32[768]{0:T(1024)}) all-reduce(f32[2,768]{1,0:T(2,128)S(1)} %fusion.125, ...), channel_id=1, replica_groups=mesh['dp'=16,'tensor'=2] {'dp','tensor'}, use_global_device_ids=true, to_apply=%region_44.45 | all-reduce | flops 9216 | bytes 73728 | tf_op jit(solution)/shard_map/psum | solution.py:316
  899.8 31.1 %all-reduce.4.cloned.1.call-done = f32[3,768,384]{2,0,1:T(4,128)} async-done(((f32[3,768,384]{2,0,1:T(4,128)}), f32[3,768,384]{2,0,1:T(4,128)}) %all-reduce.4.cloned.1.call-update) | async-done | bytes 3538960
  932.6 26.5 %reduce-scatter.22.cloned.1.call-done = bf16[512,768]{1,0:T(8,128)(2,1)} async-done(((bf16[1024,768]{1,0:T(8,128)(2,1)}), bf16[512,768]{1,0:T(8,128)(2,1)}) %reduce-scatter.22.cloned.1.call-update) | async-done | bytes 786448 | tf_op jit(solution)/shard_map/reduce_scatter | solution.py:275
  961.5 25.9 %reduce-scatter.26.cloned.1.call-done = bf16[512,768]{1,0:T(8,128)(2,1)} async-done(((bf16[1024,768]{1,0:T(8,128)(2,1)}), bf16[512,768]{1,0:T(8,128)(2,1)}) %reduce-scatter.26.cloned.1.call-update) | async-done | bytes 786448 | tf_op jit(solution)/shard_map/reduce_scatter | solution.py:275
  990.6 76.7 %reduce-scatter.32.cloned.1.call-done = f32[1536,48]{0,1:T(8,128)} async-done(((f32[1536,768]{0,1:T(8,128)}), f32[1536,48]{0,1:T(8,128)}) %reduce-scatter.32.cloned.1.call-update) | async-done | bytes 294928 | tf_op jit(solution)/shard_map/reduce_scatter | solution.py:298
  1067.4 79.2 %reduce-scatter.30.cloned.1.call-done = f32[48,1536]{1,0:T(8,128)} async-done(((f32[768,1536]{1,0:T(8,128)}), f32[48,1536]{1,0:T(8,128)}) %reduce-scatter.30.cloned.1.call-update) | async-done | bytes 294928 | tf_op jit(solution)/shard_map/reduce_scatter | solution.py:297
  1146.6 61.6 %reduce-scatter.28.cloned.1.call-done = f32[384,48]{0,1:T(8,128)} async-done(((f32[384,768]{0,1:T(8,128)}), f32[384,48]{0,1:T(8,128)}) %reduce-scatter.28.cloned.1.call-update) | async-done | bytes 73744 | tf_op jit(solution)/shard_map/reduce_scatter | solution.py:296
  (439 shorter events, 258.3 us)
Async XLA Ops:
  7.2 29.3 %copy-start.80 = (f32[2,768]{1,0:T(2,128)S(1)}, f32[2,768]{1,0:T(2,128)}, u32[]{:S(2)}) copy-start(f32[2,768]{1,0:T(2,128)} %param.28) | copy-start | bytes 18436
  7.2 32.9 %all-gather.34.cloned.1.call-start = ((), (), s32[]{:S(2)}) async-start(), calls=%async_computation.29 | async-start | bytes 2359296 | tf_op jit(solution)/shard_map/all_gather | solution.py:184
  9.9 73.0 %all-gather.14.cloned.1.call-start = ((), (), s32[]{:S(2)}) async-start(), calls=%async_computation.11 | async-start | bytes 1880064 | tf_op jit(solution)/shard_map/all_gather | solution.py:179
  10.7 112.9 %all-gather.32.cloned.1.call-start = ((), (), s32[]{:S(2)}) async-start(), calls=%async_computation.28 | async-start | bytes 2359296 | tf_op jit(solution)/shard_map/all_gather | solution.py:184
  11.4 154.1 %reduce-scatter.16.cloned.1.call-start = ((), (), s32[]{:S(2)}) async-start(), calls=%async_computation.17 | async-start | bytes 4718592 | tf_op jit(solution)/shard_map/reduce_scatter | solution.py:196
  36.4 83.3 %copy-start.29 = (bf16[384,768]{0,1:T(8,128)(2,1)}, bf16[384,768]{0,1:T(8,128)(2,1)S(1)}, u32[]{:S(2)}) copy-start(bf16[384,768]{0,1:T(8,128)(2,1)S(1)} %all_gather.42) | copy-start | bytes 1769476
  116.9 6.3 copy-start.4
  116.9 6.3 copy-start.8
  116.9 6.3 copy-start.11
  117.0 6.3 copy-start.49
  123.3 88.4 %reduce-scatter.12.cloned.1.call-start = ((), (), s32[]{:S(2)}) async-start(), calls=%async_computation.12 | async-start | bytes 4718592 | tf_op jit(solution)/shard_map/reduce_scatter | solution.py:196
  164.2 47.4 %copy-start.77 = (f32[768]{0:T(1024)S(1)}, f32[768]{0:T(1024)}, u32[]{:S(2)}) copy-start(f32[768]{0:T(1024)} %param.30) | copy-start | bytes 9220
  164.3 91.8 %all-gather.18.cloned.1.call-start = ((), (), s32[]{:S(2)}) async-start(), calls=%async_computation.14 | async-start | bytes 2506752 | tf_op jit(solution)/shard_map/all_gather | solution.py:181
  164.8 118.7 %all-gather.22.cloned.1.call-start = ((), (), s32[]{:S(2)}) async-start(), calls=%async_computation.18 | async-start | bytes 2359296 | tf_op jit(solution)/shard_map/all_gather | solution.py:205
  217.0 95.9 %all-gather.16.cloned.1.call-start = ((), (), s32[]{:S(2)}) async-start(), calls=%async_computation.13 | async-start | bytes 2359296 | tf_op jit(solution)/shard_map/all_gather | solution.py:205
  217.7 139.8 %all-gather.20.cloned.1.call-start = ((), (), s32[]{:S(2)}) async-start(), calls=%async_computation.15 | async-start | bytes 2506752 | tf_op jit(solution)/shard_map/all_gather | solution.py:182
  218.5 188.3 %reduce-scatter.14.cloned.1.call-start = ((), (), s32[]{:S(2)}) async-start(), calls=%async_computation.16 | async-start | bytes 4718592 | tf_op jit(solution)/shard_map/reduce_scatter | solution.py:208
  364.5 88.0 %reduce-scatter.18.cloned.1.call-start = ((), (), s32[]{:S(2)}) async-start(), calls=%async_computation.19 | async-start | bytes 4718592 | tf_op jit(solution)/shard_map/reduce_scatter | solution.py:208
  371.4 81.1 %copy-start.78 = (f32[768]{0:T(1024)S(1)}, f32[768]{0:T(1024)}, u32[]{:S(2)}) copy-start(f32[768]{0:T(1024)} %param.36) | copy-start | bytes 9220
  371.5 120.8 %all-gather.24.cloned.1.call-start = ((), (), s32[]{:S(2)}) async-start(), calls=%async_computation.20 | async-start | bytes 2359296 | tf_op jit(solution)/shard_map/all_gather | solution.py:222
  464.9 56.1 %all-gather.28.cloned.1.call-start = ((), (), s32[]{:S(2)}) async-start(), calls=%async_computation.24 | async-start | bytes 2359296 | tf_op jit(solution)/shard_map/all_gather | solution.py:222
  467.3 99.2 %reduce-scatter.20.cloned.1.call-start = ((), (), s32[]{:S(2)}) async-start(), calls=%async_computation.21 | async-start | bytes 4718592 | tf_op jit(solution)/shard_map/reduce_scatter | solution.py:234
  492.2 9.3 copy-start.81
  505.9 106.2 %reduce-scatter.24.cloned.1.call-start = ((), (), s32[]{:S(2)}) async-start(), calls=%async_computation.25 | async-start | bytes 4718592 | tf_op jit(solution)/shard_map/reduce_scatter | solution.py:234
  521.0 9.4 copy-start.82
  534.7 111.9 %all-gather.26.cloned.1.call-start = ((), (), s32[]{:S(2)}) async-start(), calls=%async_computation.22 | async-start | bytes 2359296 | tf_op jit(solution)/shard_map/all_gather | solution.py:247
  619.2 100.6 %all-gather.30.cloned.1.call-start = ((), (), s32[]{:S(2)}) async-start(), calls=%async_computation.26 | async-start | bytes 2359296 | tf_op jit(solution)/shard_map/all_gather | solution.py:247
  621.8 24.7 %copy-start.31 = (bf16[384,768]{0,1:T(8,128)(2,1)S(1)}, bf16[384,768]{0,1:T(8,128)(2,1)}, u32[]{:S(2)}) copy-start(bf16[384,768]{0,1:T(8,128)(2,1)} %copy-done.29) | copy-start | bytes 1769476
  624.0 306.9 %all-reduce.4.cloned.1.call-start = ((), (), s32[]{:S(2)}) async-start(), calls=%async_computation.33 | async-start | bytes 9437184
  655.8 6.3 copy-start
  667.1 11.5 copy-start.1
  687.4 6.3 copy-start
  698.7 12.0 copy-start.1
  704.5 6.3 copy-start.21
  729.3 6.3 copy-start.2
  740.7 11.5 copy-start.3
  760.9 6.3 copy-start.2
  772.3 12.0 copy-start.3
  813.5 6.8 copy-start.42
  813.6 6.8 copy-start.44
  813.6 145.5 %reduce-scatter.22.cloned.1.call-start = ((), (), s32[]{:S(2)}) async-start(), calls=%async_computation.23 | async-start | bytes 2359296 | tf_op jit(solution)/shard_map/reduce_scatter | solution.py:275
  820.1 167.3 %reduce-scatter.26.cloned.1.call-start = ((), (), s32[]{:S(2)}) async-start(), calls=%async_computation.27 | async-start | bytes 2359296 | tf_op jit(solution)/shard_map/reduce_scatter | solution.py:275
  825.7 241.7 %reduce-scatter.32.cloned.1.call-start = ((), (), s32[]{:S(2)}) async-start(), calls=%async_computation.32 | async-start | bytes 5013504 | tf_op jit(solution)/shard_map/reduce_scatter | solution.py:298
  834.9 311.7 %reduce-scatter.30.cloned.1.call-start = ((), (), s32[]{:S(2)}) async-start(), calls=%async_computation.31 | async-start | bytes 5013504 | tf_op jit(solution)/shard_map/reduce_scatter | solution.py:297
  845.8 362.4 %reduce-scatter.28.cloned.1.call-start = ((), (), s32[]{:S(2)}) async-start(), calls=%async_computation.30 | async-start | bytes 1253376 | tf_op jit(solution)/shard_map/reduce_scatter | solution.py:296
  856.3 102.8 %copy-start.19 = (f32[512,768]{1,0:T(8,128)S(1)}, f32[512,768]{1,0:T(8,128)}, u32[]{:S(2)}) copy-start(f32[512,768]{1,0:T(8,128)} %copy-done.18) | copy-start | bytes 4718596
  931.9 55.5 %copy-start.17 = (f32[512,768]{1,0:T(8,128)S(1)}, f32[512,768]{1,0:T(8,128)}, u32[]{:S(2)}) copy-start(f32[512,768]{1,0:T(8,128)} %copy-done.16) | copy-start | bytes 4718596
  961.5 27.2 %copy-start.28 = (f32[1,512,768]{2,1,0:T(8,128)S(1)}, f32[1,512,768]{2,1,0:T(8,128)}, u32[]{:S(2)}) copy-start(f32[1,512,768]{2,1,0:T(8,128)} %add_bitcast_fusion.2) | copy-start | bytes 4718596
  (73 other events, 202.6 us)
Sparse Core Ops, SparseCore 0:
  10.1 29.8 all-gather.33
  42.4 40.4 all-gather.13
  85.0 25.8 all-gather.31
  123.4 42.0 reduce-scatter.15
  168.2 43.4 reduce-scatter.11
  213.8 42.3 all-gather.17
  257.7 25.8 all-gather.21
  285.7 27.1 all-gather.15
  315.2 42.2 all-gather.19
  364.6 42.1 reduce-scatter.13
  409.0 43.4 reduce-scatter.17
  465.0 27.1 all-gather.23
  493.8 27.1 all-gather.27
  523.1 43.4 reduce-scatter.19
  568.6 43.4 reduce-scatter.23
  619.3 27.1 all-gather.25
  647.9 27.1 all-gather.29
  813.7 117.1 all-reduce.3
  933.1 25.9 reduce-scatter.21
  961.1 26.1 reduce-scatter.25
  991.8 75.5 reduce-scatter.31
  1071.8 74.7 reduce-scatter.29
  1150.8 57.3 reduce-scatter.27
where the time goes:
time: 1220 us
  waiting for transfers between devices  734 us (60%)
  matrix products  246 us (20%)
  other arithmetic  91.2 us (7%)
  blocking collectives  65.9 us (5%)
  local copies, waits for them, and re-layouts  59.4 us (5%)
  between operations  16.3 us (1%)
    reduce_scatter x2, waiting for transfers between devices, shards(): lax.psum_scatter(jnp.dot(active, full_down, preferred_element_type=jnp.fl...  81 us
    reduce_scatter x1, waiting for transfers between devices, shards(): lax.psum_scatter(local_grads[2], 'dp', scatter_dimension=0, tiled=True)  79.2 us
    reduce_scatter x1, waiting for transfers between devices, shards(): lax.psum_scatter(local_grads[3], 'dp', scatter_dimension=1, tiled=True)  76.7 us
    reduce_scatter x2, waiting for transfers between devices, shards(): lax.psum_scatter(lax.dot_general(grad_up, full_up, (((1,), (1,)), ((), ()...  72.6 us
    reduce_scatter x1, waiting for transfers between devices, shards(): lax.psum_scatter(local_grads[1], 'dp', scatter_dimension=1, tiled=True)  61.6 us
    reduce_scatter x2, waiting for transfers between devices, shards(): lax.psum_scatter(jnp.einsum('cle,cde->ld', grad_proj, full_qkv, preferred...  52.3 us
    all_gather x2, waiting for transfers between devices, shards(): spread = lax.all_gather(hidden_low, 'tensor', axis=0, tiled=True)  49.4 us
    reduce_scatter x2, waiting for transfers between devices, shards(): lax.psum_scatter(jnp.dot(context, full_o, preferred_element_type=jnp.floa...  46.3 us
  transfers between devices with their start and end apart: 23, of which 21 were waited for; matrix products, arithmetic and copies ran while one was open for 22% of the time, Pallas kernels for 0%

commit v1 on v0

--- a/solution.py
+++ b/solution.py
@@ -1,3 +1,4 @@
+import functools
 import math
 import jax
 import jax.numpy as jnp
@@ -6,6 +7,39 @@
 
 HEAD_DIM = 64
 EPS = 1e-06
+
+
+def pieces_all_start(block_in, dim_k):
+    b_next = list(block_in.shape[1:])
+    b_next[dim_k] *= block_in.shape[0]
+    r1 = jnp.moveaxis(block_in, 0, dim_k).reshape(b_next)
+    return r1
+
+
+def _register_ladders(my_tile, ax_name, out_dim):
+    k_all = jax.lax.axis_size(ax_name)
+    block_last = range(k_all)
+    row_out = map(lambda p: (p, (p + 1) % k_all), block_last)
+    views = list(row_out)
+    in_order = [(ii, i0) for i0, ii in views]
+    oldest, v1 = ([], [])
+    for rr in range(k_all - 1):
+        if rr % 2 == 0:
+            t1 = jax.lax.ppermute(oldest[-1] if oldest else my_tile, ax_name, views)
+            oldest.append(t1)
+        else:
+            current_value = jax.lax.ppermute(v1[-1] if v1 else my_tile, ax_name, in_order)
+            v1.append(current_value)
+    t_next = jnp.stack([*oldest[::-1], my_tile, *v1], axis=0)
+    earlier = jax.lax.axis_index(ax_name)
+    w_next = len(oldest)
+    next_value = earlier - w_next
+    t_next = t_next[(jnp.arange(k_all) - next_value) % k_all]
+    reached = pieces_all_start(t_next, out_dim)
+    return reached
+
+
+clear_packet = functools.partial(_register_ladders, ax_name="dp", out_dim=0)
 
 
 def gelu_exact(v):
@@ -178,7 +212,7 @@
         keep_full = keep_mask[micro_index, 0]
         full_qkv = lax.all_gather(w_qkv, "dp", axis=1, tiled=True)
         full_o = lax.all_gather(w_o, "dp", axis=1, tiled=True)
-        full_up = lax.all_gather(w_up, "dp", axis=0, tiled=True)
+        full_up = clear_packet(w_up)
         full_down = lax.all_gather(w_down, "dp", axis=1, tiled=True)
         head_count = full_qkv.shape[2] // HEAD_DIM
         gathered = lax.all_gather(own_rows, "tensor", axis=0, tiled=True)

time: 1220 us -> 1190 us (0.975)
  waiting for transfers between devices: 734 us -> 635 us
  starting transfers between devices: 1.94 us -> 34.7 us
  local copies, waits for them, and re-layouts: 59.4 us -> 86 us
    all_gather x2, waiting for transfers between devices: 49.4 us -> 0.01 us  [shards(): spread = lax.all_gather(hidden_low, 'tensor', axis=0, tiled=True)]
    all_gather x1 -> x0, waiting for transfers between devices: 37.5 us -> none  [shards(): full_up = lax.all_gather(w_up, 'dp', axis=0, tiled=True)]
    all_gather x1, waiting for transfers between devices: 33.6 us -> 0.01 us  [shards(): full_down = lax.all_gather(w_down, 'dp', axis=1, tiled=True)]
    ppermute x0 -> x15, starting transfers between devices: none -> 32.4 us  [the longest x7 32.3 us: _register_ladders(): jax.lax.ppermute(v1[-1] if v1 else my_tile, ax_name, in_order)]
    ppermute x0 -> x15, waiting for transfers between devices: none -> 26.1 us  [the longest x8 23.6 us: _register_ladders(): t1 = jax.lax.ppermute(oldest[-1] if oldest else my_tile, ax_name, views)]
    unnamed x179 -> x208, local copies, waits for them, and re-layouts: 20.1 us -> 40 us
    unnamed x24 -> x23, waiting for transfers between devices: 34.7 us -> 32 us
  transfers between devices with their start and end apart: 23 -> 37, of which waited for: 21 -> 30; matrix products, arithmetic and copies ran while one was open for 22% -> 24% of each run, Pallas kernels for 0% -> 0%
where the time goes in v1:
time: 1190 us; the launch traced here: 1180 us
  waiting for transfers between devices  635 us (53%)
  matrix products  245 us (21%)
  other arithmetic  92.9 us (8%)
  local copies, waits for them, and re-layouts  86 us (7%)
  blocking collectives  66 us (6%)
  starting transfers between devices  34.7 us (3%)
  between operations  16.4 us (1%)
    reduce_scatter x1, waiting for transfers between devices, shards(): lax.psum_scatter(local_grads[2], 'dp', scatter_dimension=0, tiled=True)  79.2 us
    reduce_scatter x2, waiting for transfers between devices, shards(): lax.psum_scatter(jnp.dot(active, full_down, preferred_element_type=jnp.fl...  78.9 us
    reduce_scatter x1, waiting for transfers between devices, shards(): lax.psum_scatter(local_grads[3], 'dp', scatter_dimension=1, tiled=True)  76.6 us
    reduce_scatter x2, waiting for transfers between devices, shards(): lax.psum_scatter(lax.dot_general(grad_up, full_up, (((1,), (1,)), ((), ()...  72.7 us
    reduce_scatter x1, waiting for transfers between devices, shards(): lax.psum_scatter(local_grads[1], 'dp', scatter_dimension=1, tiled=True)  61.5 us
    reduce_scatter x2, waiting for transfers between devices, shards(): lax.psum_scatter(jnp.einsum('cle,cde->ld', grad_proj, full_qkv, preferred...  52.3 us
    reduce_scatter x2, waiting for transfers between devices, shards(): lax.psum_scatter(jnp.dot(context, full_o, preferred_element_type=jnp.floa...  46.8 us
    all_gather x1, waiting for transfers between devices, shards(): full_qkv = lax.all_gather(w_qkv, 'dp', axis=1, tiled=True)  42.8 us
  transfers between devices with their start and end apart: 37, of which 30 were waited for; matrix products, arithmetic and copies ran while one was open for 24% of the time, Pallas kernels for 0%

profile of v1, /device:TPU:0, one launch (start us, length us, event | category | flops | bytes accessed | tf_op | source)
XLA Modules:
  0.0 1177.2 jit_solution(9076344275766372239)
XLA Ops:
  11.5 24.9 %all_gather.38 = bf16[384,768]{0,1:T(8,128)(2,1)S(1)} all-gather(bf16[384,48]{0,1:T(8,128)(2,1)S(1)} %copy-done.67), channel_id=1, replica_groups=mesh['dp'=16,'tensor'=2] {'dp'}, dimensions={1}, use_global_device_ids=true | all-gather | bytes 626688 | tf_op jit(solution)/shard_map/all_gather | solution.py:214
  40.1 42.8 %all-gather.13.cloned.1.call-done = bf16[3,768,384]{2,1,0:T(8,128)(2,1)} async-done(((bf16[3,48,384]{2,1,0:T(8,128)(2,1)}), bf16[3,768,384]{2,1,0:T(8,128)(2,1)}) %all-gather.13.cloned.1.call-update) | async-done | bytes 1769488 | tf_op jit(solution)/shard_map/all_gather | solution.py:213
  90.9 26.0 %while.55 = (s32[]{:T(128)}, bf16[2,512,6,64]{1,3,2,0:T(8,128)(2,1)}, f32[2,6,512]{2,1,0:T(8,128)S(1)}, s32[2,512]{1,0:T(2,128)S(1)}, s32[1,1,1024]{2,1,0:T(1,12...) while((s32[]{:T(128)}, ...), condition=%wide.region_13.14_spmd, body=%wide.region_10.13_spmd.sunk | while | flops 845347328 | bytes 42336904 | solution.py:107
  132.2 26.0 %while.54 = (s32[]{:T(128)}, bf16[2,512,6,64]{1,3,2,0:T(8,128)(2,1)}, f32[2,6,512]{2,1,0:T(8,128)S(1)}, s32[2,512]{1,0:T(2,128)S(1)}, s32[1,1,1024]{2,1,0:T(1,12...) while((s32[]{:T(128)}, ...), condition=%wide.region_3.4_spmd, body=%wide.region_0.3_spmd.sunk | while | flops 845347328 | bytes 42336904 | solution.py:107
  165.5 46.1 %reduce-scatter.12.cloned.1.call-done = f32[512,768]{1,0:T(8,128)} async-done(((f32[1024,768]{1,0:T(8,128)}), f32[512,768]{1,0:T(8,128)}) %reduce-scatter.12.cloned.1.call-update) | async-done | bytes 1572880 | tf_op jit(solution)/shard_map/reduce_scatter | solution.py:230
  217.9 7.3 collective-permute-done
  300.9 7.4 fusion.151
  308.3 11.2 multiply_convert_fusion.3
  319.5 6.9 fusion.149
  326.5 6.9 fusion.152
  333.6 33.4 %reduce-scatter.14.cloned.1.call-done = f32[512,768]{1,0:T(8,128)} async-done(((f32[1024,768]{1,0:T(8,128)}), f32[512,768]{1,0:T(8,128)}) %reduce-scatter.14.cloned.1.call-update) | async-done | bytes 1572880 | tf_op jit(solution)/shard_map/reduce_scatter | solution.py:242
  367.0 45.6 %reduce-scatter.18.cloned.1.call-done = f32[512,768]{1,0:T(8,128)} async-done(((f32[1024,768]{1,0:T(8,128)}), f32[512,768]{1,0:T(8,128)}) %reduce-scatter.18.cloned.1.call-update) | async-done | bytes 1572880 | tf_op jit(solution)/shard_map/reduce_scatter | solution.py:242
  427.4 24.9 %all-gather.21.cloned.1.call-done = bf16[1024,768]{1,0:T(8,128)(2,1)} async-done(((bf16[512,768]{1,0:T(8,128)(2,1)}), bf16[1024,768]{1,0:T(8,128)(2,1)}) %all-gather.21.cloned.1.call-update) | async-done | bytes 1572880 | tf_op jit(solution)/shard_map/all_gather | solution.py:256
  452.3 7.7 convert_reduce_fusion.1
  466.0 14.8 %all-gather.25.cloned.1.call-done = bf16[1024,768]{1,0:T(8,128)(2,1)} async-done(((bf16[512,768]{1,0:T(8,128)(2,1)}), bf16[1024,768]{1,0:T(8,128)(2,1)}) %all-gather.25.cloned.1.call-update) | async-done | bytes 1572880 | tf_op jit(solution)/shard_map/all_gather | solution.py:256
  480.9 7.7 convert_reduce_fusion
  494.7 31.9 %reduce-scatter.20.cloned.1.call-done = f32[512,768]{1,0:T(8,128)} async-done(((f32[1024,768]{1,0:T(8,128)}), f32[512,768]{1,0:T(8,128)}) %reduce-scatter.20.cloned.1.call-update) | async-done | bytes 1572880 | tf_op jit(solution)/shard_map/reduce_scatter | solution.py:268
  531.3 40.8 %reduce-scatter.24.cloned.1.call-done = f32[512,768]{1,0:T(8,128)} async-done(((f32[1024,768]{1,0:T(8,128)}), f32[512,768]{1,0:T(8,128)}) %reduce-scatter.24.cloned.1.call-update) | async-done | bytes 1572880 | tf_op jit(solution)/shard_map/reduce_scatter | solution.py:268
  584.3 22.5 %all-gather.23.cloned.1.call-done = bf16[1024,768]{1,0:T(8,128)(2,1)} async-done(((bf16[512,768]{1,0:T(8,128)(2,1)}), bf16[1024,768]{1,0:T(8,128)(2,1)}) %all-gather.23.cloned.1.call-update) | async-done | bytes 1572880 | tf_op jit(solution)/shard_map/all_gather | solution.py:281
  612.0 65.1 %while.56 = (s32[]{:T(128)}, f32[1024,6,64]{0,2,1:T(8,128)}, f32[1024,6,64]{0,2,1:T(8,128)}, bf16[2,512,6,64]{1,3,2,0:T(8,128)(2,1)}, bf16[2,512,6,64]{1,3,2,0:T...) while((s32[]{:T(128)}, f32[1024,6,64]{0,2,1:T(8,128)}, ...), condition=%wide.region_27.28_spmd.clone, body=%wide.region_25.27_spmd.clone.sunk | while | flops 2064906752 | bytes 211006768 | solution.py:152
  616.2 6.3 multiply_reduce_fusion.14
  622.5 5.1 multiply_convert_fusion.6
  627.5 5.3 bitcast_add_fusion.8
  632.9 6.2 fusion.271
  647.8 6.3 multiply_reduce_fusion.14
  654.1 5.1 multiply_convert_fusion.6
  659.1 5.7 bitcast_add_fusion.8
  664.9 6.2 fusion.271
  671.1 6.0 bitcast_add_fusion.9
  685.4 65.1 %while.57 = (s32[]{:T(128)}, f32[1024,6,64]{0,2,1:T(8,128)}, f32[1024,6,64]{0,2,1:T(8,128)}, bf16[2,512,6,64]{1,3,2,0:T(8,128)(2,1)}, bf16[2,512,6,64]{1,3,2,0:T...) while((s32[]{:T(128)}, f32[1024,6,64]{0,2,1:T(8,128)}, ...), condition=%wide.region_36.37_spmd.clone, body=%wide.region_34.36_spmd.clone.sunk | while | flops 2064906752 | bytes 211006768 | solution.py:152
  689.4 6.3 multiply_reduce_fusion.15
  695.7 5.1 multiply_convert_fusion.7
  700.8 5.3 bitcast_add_fusion.10
  706.1 6.2 fusion.283
  721.1 6.3 multiply_reduce_fusion.15
  727.3 5.1 multiply_convert_fusion.7
  732.4 5.7 bitcast_add_fusion.10
  738.1 6.2 fusion.283
  744.4 6.0 bitcast_add_fusion.11
  777.3 5.1 bitcast_convert_fusion.1
  782.9 5.2 bitcast_convert_fusion
  821.1 41.1 %all-reduce.1 = (f32[2,768]{1,0:T(2,128)S(1)}, f32[768]{0:T(1024)}, f32[768]{0:T(1024)}, f32[768]{0:T(1024)}, f32[3072]{0:T(1024)S(1)}, /*index=5*/f32[768]{0:T(1024)}, f32[768]{0:T(1024)}, f32[768]{0:T(1024)}) all-reduce(f32[2,768]{1,0:T(2,128)S(1)} %fusion.125, ...), channel_id=1, replica_groups=mesh['dp'=16,'tensor'=2] {'dp','tensor'}, use_global_device_ids=true, to_apply=%region_44.45 | all-reduce | flops 9216 | bytes 73728 | tf_op jit(solution)/shard_map/psum | solution.py:350
  863.5 29.6 %all-reduce.4.cloned.1.call-done = f32[3,768,384]{2,0,1:T(4,128)} async-done(((f32[3,768,384]{2,0,1:T(4,128)}), f32[3,768,384]{2,0,1:T(4,128)}) %all-reduce.4.cloned.1.call-update) | async-done | bytes 3538960
  894.8 26.3 %reduce-scatter.22.cloned.1.call-done = bf16[512,768]{1,0:T(8,128)(2,1)} async-done(((bf16[1024,768]{1,0:T(8,128)(2,1)}), bf16[512,768]{1,0:T(8,128)(2,1)}) %reduce-scatter.22.cloned.1.call-update) | async-done | bytes 786448 | tf_op jit(solution)/shard_map/reduce_scatter | solution.py:309
  923.6 26.0 %reduce-scatter.26.cloned.1.call-done = bf16[512,768]{1,0:T(8,128)(2,1)} async-done(((bf16[1024,768]{1,0:T(8,128)(2,1)}), bf16[512,768]{1,0:T(8,128)(2,1)}) %reduce-scatter.26.cloned.1.call-update) | async-done | bytes 786448 | tf_op jit(solution)/shard_map/reduce_scatter | solution.py:309
  952.9 76.6 %reduce-scatter.32.cloned.1.call-done = f32[1536,48]{0,1:T(8,128)} async-done(((f32[1536,768]{0,1:T(8,128)}), f32[1536,48]{0,1:T(8,128)}) %reduce-scatter.32.cloned.1.call-update) | async-done | bytes 294928 | tf_op jit(solution)/shard_map/reduce_scatter | solution.py:332
  1029.4 79.2 %reduce-scatter.30.cloned.1.call-done = f32[48,1536]{1,0:T(8,128)} async-done(((f32[768,1536]{1,0:T(8,128)}), f32[48,1536]{1,0:T(8,128)}) %reduce-scatter.30.cloned.1.call-update) | async-done | bytes 294928 | tf_op jit(solution)/shard_map/reduce_scatter | solution.py:331
  1108.7 61.5 %reduce-scatter.28.cloned.1.call-done = f32[384,48]{0,1:T(8,128)} async-done(((f32[384,768]{0,1:T(8,128)}), f32[384,48]{0,1:T(8,128)}) %reduce-scatter.28.cloned.1.call-update) | async-done | bytes 73744 | tf_op jit(solution)/shard_map/reduce_scatter | solution.py:330
  (499 shorter events, 322.2 us)
Async XLA Ops:
  7.2 29.3 %copy-start.89 = (f32[2,768]{1,0:T(2,128)S(1)}, f32[2,768]{1,0:T(2,128)}, u32[]{:S(2)}) copy-start(f32[2,768]{1,0:T(2,128)} %param.28) | copy-start | bytes 18436
  7.2 32.9 %all-gather.31.cloned.1.call-start = ((), (), s32[]{:S(2)}) async-start(), calls=%async_computation.28 | async-start | bytes 2359296 | tf_op jit(solution)/shard_map/all_gather | solution.py:218
  9.9 73.0 %all-gather.13.cloned.1.call-start = ((), (), s32[]{:S(2)}) async-start(), calls=%async_computation.11 | async-start | bytes 1880064 | tf_op jit(solution)/shard_map/all_gather | solution.py:213
  10.7 113.0 %all-gather.29.cloned.1.call-start = ((), (), s32[]{:S(2)}) async-start(), calls=%async_computation.27 | async-start | bytes 2359296 | tf_op jit(solution)/shard_map/all_gather | solution.py:218
  11.4 154.1 %reduce-scatter.16.cloned.1.call-start = ((), (), s32[]{:S(2)}) async-start(), calls=%async_computation.16 | async-start | bytes 4718592 | tf_op jit(solution)/shard_map/reduce_scatter | solution.py:230
  36.4 83.3 %copy-start.29 = (bf16[384,768]{0,1:T(8,128)(2,1)}, bf16[384,768]{0,1:T(8,128)(2,1)S(1)}, u32[]{:S(2)}) copy-start(bf16[384,768]{0,1:T(8,128)(2,1)S(1)} %all_gather.38) | copy-start | bytes 1769476
  123.3 88.3 %reduce-scatter.12.cloned.1.call-start = ((), (), s32[]{:S(2)}) async-start(), calls=%async_computation.12 | async-start | bytes 4718592 | tf_op jit(solution)/shard_map/reduce_scatter | solution.py:230
  164.2 47.4 %copy-start.86 = (f32[768]{0:T(1024)S(1)}, f32[768]{0:T(1024)}, u32[]{:S(2)}) copy-start(f32[768]{0:T(1024)} %param.30) | copy-start | bytes 9220
  164.3 136.7 %all-gather.19.cloned.1.call-start = ((), (), s32[]{:S(2)}) async-start(), calls=%async_computation.17 | async-start | bytes 2359296 | tf_op jit(solution)/shard_map/all_gather | solution.py:239
  215.3 54.4 %copy-start.85 = (f32[3072]{0:T(1024)S(1)}, f32[3072]{0:T(1024)}, u32[]{:S(2)}) copy-start(f32[3072]{0:T(1024)} %param.34) | copy-start | bytes 36868
  217.0 91.3 %all-gather.15.cloned.1.call-start = ((), (), s32[]{:S(2)}) async-start(), calls=%async_computation.13 | async-start | bytes 2359296 | tf_op jit(solution)/shard_map/all_gather | solution.py:239
  217.8 101.7 %all-gather.17.cloned.1.call-start = ((), (), s32[]{:S(2)}) async-start(), calls=%async_computation.14 | async-start | bytes 2506752 | tf_op jit(solution)/shard_map/all_gather | solution.py:216
  217.8 7.3 collective-permute-start
  225.1 7.3 collective-permute-start.1
  225.1 7.3 collective-permute-start.8
  232.4 7.4 collective-permute-start.2
  233.1 7.1 collective-permute-start.9
  239.8 7.4 collective-permute-start.3
  240.2 7.4 collective-permute-start.10
  247.2 7.4 collective-permute-start.4
  247.6 7.4 collective-permute-start.11
  254.5 7.5 collective-permute-start.5
  254.9 7.8 collective-permute-start.12
  262.0 7.7 collective-permute-start.6
  262.0 105.0 %reduce-scatter.14.cloned.1.call-start = ((), (), s32[]{:S(2)}) async-start(), calls=%async_computation.15 | async-start | bytes 4718592 | tf_op jit(solution)/shard_map/reduce_scatter | solution.py:242
  262.7 7.7 collective-permute-start.13
  269.7 7.6 collective-permute-start.7
  269.7 20.6 %copy-start.60 = (bf16[48,1536]{1,0:T(8,128)(2,1)S(1)}, bf16[48,1536]{1,0:T(8,128)(2,1)}, u32[]{:S(2)}) copy-start(bf16[48,1536]{1,0:T(8,128)(2,1)} %copy-done.59) | copy-start | bytes 442372
  269.7 21.3 %copy-start.63 = (bf16[48,1536]{1,0:T(8,128)(2,1)S(1)}, bf16[48,1536]{1,0:T(8,128)(2,1)}, u32[]{:S(2)}) copy-start(bf16[48,1536]{1,0:T(8,128)(2,1)} %copy-done.62) | copy-start | bytes 442372
  270.4 26.0 %collective-permute-start.14 = (bf16[48,1536]{1,0:T(8,128)(2,1)}, bf16[48,1536]{1,0:T(8,128)(2,1)S(1)}, u32[]{:S(2)}, u32[]{:S(2)}) collective-permute-start(bf16[48,1536]{1,0:T(8,128)(2,1)} %collective-permute-done.13), channel_id=1, source_target_pairs={{2,0},{4,2},{6,4},{8,6},{10,8},{12,10},{14,12},{16,14},{18,16},{20... | collective-permute-start | bytes 442376 | tf_op jit(solution)/shard_map/ppermute | solution.py:31
  326.4 86.1 %reduce-scatter.18.cloned.1.call-start = ((), (), s32[]{:S(2)}) async-start(), calls=%async_computation.18 | async-start | bytes 4718592 | tf_op jit(solution)/shard_map/reduce_scatter | solution.py:242
  333.4 79.2 %copy-start.87 = (f32[768]{0:T(1024)S(1)}, f32[768]{0:T(1024)}, u32[]{:S(2)}) copy-start(f32[768]{0:T(1024)} %param.36) | copy-start | bytes 9220
  333.4 118.9 %all-gather.21.cloned.1.call-start = ((), (), s32[]{:S(2)}) async-start(), calls=%async_computation.19 | async-start | bytes 2359296 | tf_op jit(solution)/shard_map/all_gather | solution.py:256
  424.9 56.0 %all-gather.25.cloned.1.call-start = ((), (), s32[]{:S(2)}) async-start(), calls=%async_computation.23 | async-start | bytes 2359296 | tf_op jit(solution)/shard_map/all_gather | solution.py:256
  427.4 99.2 %reduce-scatter.20.cloned.1.call-start = ((), (), s32[]{:S(2)}) async-start(), calls=%async_computation.20 | async-start | bytes 4718592 | tf_op jit(solution)/shard_map/reduce_scatter | solution.py:268
  466.0 106.2 %reduce-scatter.24.cloned.1.call-start = ((), (), s32[]{:S(2)}) async-start(), calls=%async_computation.24 | async-start | bytes 4718592 | tf_op jit(solution)/shard_map/reduce_scatter | solution.py:268
  494.7 112.1 %all-gather.23.cloned.1.call-start = ((), (), s32[]{:S(2)}) async-start(), calls=%async_computation.21 | async-start | bytes 2359296 | tf_op jit(solution)/shard_map/all_gather | solution.py:281
  579.4 100.7 %all-gather.27.cloned.1.call-start = ((), (), s32[]{:S(2)}) async-start(), calls=%async_computation.25 | async-start | bytes 2359296 | tf_op jit(solution)/shard_map/all_gather | solution.py:281
  582.0 24.7 %copy-start.31 = (bf16[384,768]{0,1:T(8,128)(2,1)S(1)}, bf16[384,768]{0,1:T(8,128)(2,1)}, u32[]{:S(2)}) copy-start(bf16[384,768]{0,1:T(8,128)(2,1)} %copy-done.29) | copy-start | bytes 1769476
  584.2 308.9 %all-reduce.4.cloned.1.call-start = ((), (), s32[]{:S(2)}) async-start(), calls=%async_computation.32 | async-start | bytes 9437184
  775.9 145.2 %reduce-scatter.22.cloned.1.call-start = ((), (), s32[]{:S(2)}) async-start(), calls=%async_computation.22 | async-start | bytes 2359296 | tf_op jit(solution)/shard_map/reduce_scatter | solution.py:309
  782.4 167.2 %reduce-scatter.26.cloned.1.call-start = ((), (), s32[]{:S(2)}) async-start(), calls=%async_computation.26 | async-start | bytes 2359296 | tf_op jit(solution)/shard_map/reduce_scatter | solution.py:309
  788.1 241.4 %reduce-scatter.32.cloned.1.call-start = ((), (), s32[]{:S(2)}) async-start(), calls=%async_computation.31 | async-start | bytes 5013504 | tf_op jit(solution)/shard_map/reduce_scatter | solution.py:332
  797.3 311.3 %reduce-scatter.30.cloned.1.call-start = ((), (), s32[]{:S(2)}) async-start(), calls=%async_computation.30 | async-start | bytes 5013504 | tf_op jit(solution)/shard_map/reduce_scatter | solution.py:331
  808.1 362.1 %reduce-scatter.28.cloned.1.call-start = ((), (), s32[]{:S(2)}) async-start(), calls=%async_computation.29 | async-start | bytes 1253376 | tf_op jit(solution)/shard_map/reduce_scatter | solution.py:330
  817.1 104.0 %copy-start.19 = (f32[512,768]{1,0:T(8,128)S(1)}, f32[512,768]{1,0:T(8,128)}, u32[]{:S(2)}) copy-start(f32[512,768]{1,0:T(8,128)} %copy-done.18) | copy-start | bytes 4718596
  894.1 55.5 %copy-start.17 = (f32[512,768]{1,0:T(8,128)S(1)}, f32[512,768]{1,0:T(8,128)}, u32[]{:S(2)}) copy-start(f32[512,768]{1,0:T(8,128)} %copy-done.16) | copy-start | bytes 4718596
  923.6 27.3 %copy-start.28 = (f32[1,512,768]{2,1,0:T(8,128)S(1)}, f32[1,512,768]{2,1,0:T(8,128)}, u32[]{:S(2)}) copy-start(f32[1,512,768]{2,1,0:T(8,128)} %add_bitcast_fusion.2) | copy-start | bytes 4718596
  (94 other events, 411.7 us)
Sparse Core Ops, SparseCore 0:
  10.1 29.8 all-gather.30
  42.4 40.4 all-gather.12
  85.0 25.8 all-gather.28
  123.4 42.0 reduce-scatter.15
  168.2 43.3 reduce-scatter.11
  217.1 27.1 all-gather.18
  245.9 27.1 all-gather.14
  275.4 42.2 all-gather.16
  326.5 40.3 reduce-scatter.13
  369.1 43.4 reduce-scatter.17
  425.0 27.1 all-gather.20
  453.7 27.1 all-gather.24
  483.1 43.4 reduce-scatter.19
  528.7 43.4 reduce-scatter.23
  579.5 27.1 all-gather.22
  608.2 27.1 all-gather.26
  776.0 116.9 all-reduce.3
  895.2 25.9 reduce-scatter.21
  923.4 26.1 reduce-scatter.25
  953.8 75.5 reduce-scatter.31
  1033.9 74.7 reduce-scatter.29
  1112.8 57.3 reduce-scatter.27
